TPU v7x, 32 devices: a whole 2x2x4 slice. The times are simulated.
32 devices in a mesh: blk: 8 (over y, x, core), uly: 1, dp: 4 (over z).
Axes of the slice: x: 2, y: 2, z: 4, core: 2. Of those that a mesh axis runs over, the one named last changes fastest.
Arguments:
- short_tokens: bfloat16 [32, 1024, 4096], P(('blk', 'dp'), 'uly'), may hold values from -150 to 150, as said below
- short_segments: int32 [32, 1024], P(('blk', 'dp')), may hold values from 0 to 3, never falling along the last dimension, each value on 1 to 512 neighbouring positions
- long_tokens: bfloat16 [4, 3072, 4096], P('dp', 'blk'), may hold values from -150 to 150, as said below
- long_lengths: int32 [4], P('dp'), may hold values from 768 to 3072
- w_query: bfloat16 [4096, 2048], P(('blk', 'dp'), 'uly'), may hold values from -0.09375 to 0.09375
- w_key: bfloat16 [4096, 512], P(('blk', 'dp'), 'uly'), may hold values from -0.09375 to 0.09375
- w_value: bfloat16 [4096, 512], P(('blk', 'dp'), 'uly'), may hold values from -0.09375 to 0.09375
Outputs:
- short_out: bfloat16 [32, 1024, 2048], P(('blk', 'dp'), 'uly')
- long_out: bfloat16 [4, 3072, 2048], P('dp', 'blk', 'uly')
Inputs may be any that keep to these rules, and one draw needn't show every extreme that they name: `short_tokens`: activations of the short bucket. `long_tokens`: activations of the long bucket; rows at or after a sequence's length are padding. `short_segments`: document numbers never fall along a sequence. `long_lengths`: a long sequence occupies positions 0 to its length - 1 of its 3072 slots.
All inputs are finite; a program needn't handle non-finite values.
Results may differ from a plain program's by a relative error of at most 0.012.
The roundings to bfloat16 on the way count: a program that leaves them out, or rounds other values in their place, can miss the bound.
Values may be sent and summed in bfloat16 or wider, within the bound.
A program may use at most 128 MiB of HBM per device.

v0:
```python
import math
import jax
import jax.numpy as jnp
from jax import lax
from jax.sharding import PartitionSpec as P

HD = 128
masked_score = -1e30


def head_scores(query_rows, key_rows, kv_heads):
    query_heads = query_rows.reshape(query_rows.shape[0], kv_heads, -1, HD)
    key_heads = key_rows.reshape(key_rows.shape[0], kv_heads, HD)
    scores = jnp.einsum(
        "bhgd,khd->hgbk", query_heads, key_heads, preferred_element_type=jnp.float32
    )
    return scores * (1.0 / math.sqrt(HD))


def weighted_values(probabilities, value_rows, kv_heads):
    value_heads = value_rows.reshape(value_rows.shape[0], kv_heads, HD)
    return jnp.einsum(
        "hgbk,khd->hgbd", probabilities, value_heads, preferred_element_type=jnp.float32
    )


def short_attention(queries, key_rows, value_rows, segments):
    kv_heads = key_rows.shape[1] // HD
    seq_len = key_rows.shape[0]
    block_rows = min(512, seq_len)
    positions = jnp.arange(seq_len, dtype=jnp.int32)
    outputs = []
    for block_index in range(seq_len // block_rows):
        first_row = block_index * block_rows
        query_pos = positions[first_row : first_row + block_rows]
        query_seg = segments[first_row : first_row + block_rows]
        visible = (positions[None, :] <= query_pos[:, None]) & (
            segments[None, :] == query_seg[:, None]
        )
        scores = head_scores(queries[first_row : first_row + block_rows], key_rows, kv_heads)
        scores = jnp.where(visible, scores, masked_score)
        row_max = jnp.max(scores, axis=-1, keepdims=True)
        exponentials = jnp.where(visible, jnp.exp(scores - row_max), 0.0)
        totals = jnp.sum(exponentials, axis=-1)
        mixed = (
            weighted_values(exponentials.astype(jnp.bfloat16), value_rows, kv_heads)
            / totals[..., None]
        )
        outputs.append(jnp.transpose(mixed, (2, 0, 1, 3)).reshape(block_rows, -1))
    return jnp.concatenate(outputs, axis=0).astype(jnp.bfloat16)


def local(short_tokens, short_segments, long_tokens, long_lengths, w_query, w_key, w_value):
    short_rows = short_tokens[0]
    long_rows = long_tokens[0]
    long_count = long_rows.shape[0]
    query_cols = w_query.shape[1]
    kv_cols = w_key.shape[1]
    whole_rows = lax.all_gather(short_rows, "uly", axis=0, tiled=True)
    pieces = (
        lax.all_gather(w_query, ("blk", "dp"), axis=0, tiled=True),
        lax.all_gather(w_key, ("blk", "dp"), axis=0, tiled=True),
        lax.all_gather(w_value, ("blk", "dp"), axis=0, tiled=True),
    )
    short_new = tuple(
        (jnp.dot(whole_rows, pieces[i], preferred_element_type=jnp.float32) for i in range(3))
    )
    long_new = tuple(
        (jnp.dot(long_rows, pieces[i], preferred_element_type=jnp.float32) for i in range(3))
    )
    projected = short_new + long_new
    query_short, key_short, value_short = tuple(
        (item.astype(jnp.bfloat16) for item in projected[:3])
    )
    query_long, key_long, value_long = tuple((item.astype(jnp.bfloat16) for item in projected[3:]))
    attended = short_attention(query_short, key_short, value_short, short_segments[0])
    short_back = lax.all_to_all(attended, "uly", split_axis=0, concat_axis=1, tiled=True)
    long_len = long_lengths[0]
    query_pos = lax.axis_index("blk") * long_count + jnp.arange(long_count, dtype=jnp.int32)
    kv_heads = kv_cols // HD
    group_size = query_cols // kv_cols
    cycle_init = (
        jnp.full((kv_heads, group_size, long_count), masked_score, jnp.float32),
        jnp.zeros((kv_heads, group_size, long_count), jnp.float32),
        jnp.zeros((kv_heads, group_size, long_count, HD), jnp.float32),
    )
    carry = cycle_init
    key_piece = lax.all_gather(key_long, "blk", axis=0, tiled=True)
    value_piece = lax.all_gather(value_long, "blk", axis=0, tiled=True)
    piece_rows = key_piece.shape[0]
    block_rows = math.gcd(piece_rows, 512)
    blocks_count = piece_rows // block_rows
    key_blocks = key_piece.reshape(blocks_count, block_rows, -1)
    value_blocks = value_piece.reshape(blocks_count, block_rows, -1)
    block_starts = block_rows * jnp.arange(blocks_count, dtype=jnp.int32)

    def update(states, block_key, block_value, block_start):
        running_max, running_sum, accumulated = states
        key_pos = block_start + jnp.arange(block_rows, dtype=jnp.int32)
        visible = (key_pos[None, :] <= query_pos[:, None]) & (key_pos[None, :] < long_len)
        scores = jnp.where(visible, head_scores(query_long, block_key, kv_heads), masked_score)
        new_max = jnp.maximum(running_max, jnp.max(scores, axis=-1))
        rescale = jnp.exp(running_max - new_max)
        exponentials = jnp.where(visible, jnp.exp(scores - new_max[..., None]), 0.0)
        running_sum = running_sum * rescale + jnp.sum(exponentials, axis=-1)
        accumulated = accumulated * rescale[..., None] + weighted_values(
            exponentials.astype(jnp.bfloat16), block_value, kv_heads
        )
        return (new_max, running_sum, accumulated)

    def advance(states, inputs):
        block_key, block_value, block_start = inputs
        states = update(states, block_key, block_value, block_start)
        return (states, None)

    carry, unused = lax.scan(advance, carry, (key_blocks, value_blocks, block_starts))
    running_max, running_sum, accumulated = carry
    mixed = accumulated / running_sum[..., None]
    mixed = jnp.transpose(mixed, (2, 0, 1, 3)).reshape(long_count, query_cols)
    mixed = jnp.where(query_pos[:, None] < long_len, mixed, 0.0)
    return (short_back[None], mixed.astype(jnp.bfloat16)[None])


def solution(mesh):
    return jax.shard_map(
        local,
        mesh=mesh,
        in_specs=(
            P(("blk", "dp"), "uly", None),
            P(("blk", "dp"), None),
            P("dp", "blk", None),
            P("dp"),
            P(("blk", "dp"), "uly"),
            P(("blk", "dp"), "uly"),
            P(("blk", "dp"), "uly"),
        ),
        out_specs=(P(("blk", "dp"), "uly", None), P("dp", "blk", "uly")),
        check_vma=False,
    )
```

profile of v0, /device:TPU:0, one launch (start us, length us, event | category | flops | bytes accessed | tf_op | source)
XLA Modules:
  0.0 508.8 jit_solution(50371150435943423)
XLA Ops:
  8.0 0.7 all-gather.6.cloned.1.call-update
  9.5 65.9 %all-gather.10.cloned.1.call-done = bf16[4096,512]{1,0:T(8,128)(2,1)} async-done(((bf16[128,512]{1,0:T(8,128)(2,1)}), bf16[4096,512]{1,0:T(8,128)(2,1)}) %all-gather.10.cloned.1.call-update) | async-done | bytes 4194320 | tf_op jit(solution)/shard_map/all_gather | solution.py:63
  75.4 4.7 fusion.84
  81.4 1.9 fusion.59
  83.3 55.5 %all-gather.6.cloned.1.call-done = bf16[4096,512]{1,0:T(8,128)(2,1)} async-done(((bf16[128,512]{1,0:T(8,128)(2,1)}), bf16[4096,512]{1,0:T(8,128)(2,1)}) %all-gather.6.cloned.1.call-update) | async-done | bytes 4194320 | tf_op jit(solution)/shard_map/all_gather | solution.py:62
  138.8 4.7 fusion.81
  143.6 10.3 %fusion.78 = bf16[1024,512]{0,1:T(8,128)(2,1)} fusion(bf16[4096,512]{1,0:T(8,128)(2,1)} %all-gather.10.cloned.1.call-done, bf16[1,1024,4096]{2,1,0:T(8,128)(2,1)} %param.9), kind=kOutput, calls=%fused_computation.77 | convolution fusion | flops 4295491584 | bytes 13631488 | tf_op jit(solution)/shard_map/dot_general | solution.py:66
  153.8 8.4 %fusion.75 = bf16[1024,512]{0,1:T(8,128)(2,1)} fusion(bf16[4096,512]{1,0:T(8,128)(2,1)S(1)} %copy-done.10, bf16[1,1024,4096]{2,1,0:T(8,128)(2,1)} %param.9), kind=kOutput, calls=%fused_computation.76 | convolution fusion | flops 4295491584 | bytes 13631488 | tf_op jit(solution)/shard_map/dot_general | solution.py:66
  162.2 92.7 %all-gather.8.cloned.1.call-done = bf16[4096,2048]{1,0:T(8,128)(2,1)} async-done(((bf16[128,2048]{1,0:T(8,128)(2,1)}), bf16[4096,2048]{1,0:T(8,128)(2,1)}) %all-gather.8.cloned.1.call-update) | async-done | bytes 16777232 | tf_op jit(solution)/shard_map/all_gather | solution.py:61
  255.0 22.7 %fusion.43 = bf16[1024,2048]{1,0:T(8,128)(2,1)S(1)} fusion(bf16[4096,2048]{1,0:T(8,128)(2,1)} %all-gather.8.cloned.1.call-done, bf16[1,1024,4096]{2,1,0:T(8,128)(2,1)} %param.9), kind=kOutput, calls=%fused_computation.56 | convolution fusion | flops 17181966336 | bytes 29360128 | tf_op jit(solution)/shard_map/dot_general | solution.py:66
  277.7 2.4 fusion.91
  280.0 4.5 reshape.136
  284.5 11.6 %fusion.52 = bf16[384,2048]{1,0:T(8,128)(2,1)} fusion(bf16[4096,2048]{1,0:T(8,128)(2,1)} %all-gather.8.cloned.1.call-done, bf16[1,384,4096]{2,1,0:T(8,128)(2,1)S(1)} %copy-done), kind=kOutput, calls=%fused_computation.65 | convolution fusion | flops 6443237376 | bytes 21495808 | tf_op jit(solution)/shard_map/dot_general | solution.py:69
  296.1 2.8 reshape.150
  299.0 4.4 reshape.138
  303.4 17.7 %all-gather.12.cloned.1.call-done = bf16[3072,512]{1,0:T(8,128)(2,1)} async-done(((bf16[384,512]{1,0:T(8,128)(2,1)}), bf16[3072,512]{1,0:T(8,128)(2,1)}) %all-gather.12.cloned.1.call-update) | async-done | bytes 3145744 | tf_op jit(solution)/shard_map/all_gather | solution.py:88
  321.1 102.2 %while.16 = (s32[]{:T(128)}, f32[4,4,384]{2,1,0:T(4,128)S(1)}, f32[4,4,384]{2,1,0:T(4,128)S(1)}, f32[4,4,384,128]{3,2,1,0:T(8,128)}, s32[6]{0:T(128)S(1)}, /*ind...) while((s32[]{:T(128)}, f32[4,4,384]{2,1,0:T(4,128)S(1)}, ...), condition=%wide.wide.region_7.8_spmd.clone, body=%wide.wide.region_4.7_spmd.clone.sunk | while | flops 1654292352 | bytes 77209832 | solution.py:116
  321.9 1.3 broadcast_compare_fusion.3
  324.1 1.3 constant_dynamic-slice_fusion.4
  325.8 2.7 fusion.136
  328.5 3.0 fusion.137
  331.6 5.1 fusion.139
  336.7 1.6 copy-done.4
  338.9 1.3 broadcast_compare_fusion.3
  341.1 1.3 constant_dynamic-slice_fusion.4
  342.8 2.7 fusion.136
  345.5 3.0 fusion.137
  348.6 5.1 fusion.139
  353.7 1.6 copy-done.4
  355.9 1.3 broadcast_compare_fusion.3
  358.1 1.3 constant_dynamic-slice_fusion.4
  359.8 2.7 fusion.136
  362.5 3.0 fusion.137
  365.6 5.1 fusion.139
  370.7 1.6 copy-done.4
  372.9 1.3 broadcast_compare_fusion.3
  375.1 1.3 constant_dynamic-slice_fusion.4
  376.8 2.7 fusion.136
  379.5 3.0 fusion.137
  382.6 5.1 fusion.139
  387.7 1.6 copy-done.4
  390.0 1.3 broadcast_compare_fusion.3
  392.1 1.3 constant_dynamic-slice_fusion.4
  393.8 2.7 fusion.136
  396.5 3.0 fusion.137
  399.6 5.1 fusion.139
  404.7 1.6 copy-done.4
  407.0 1.3 broadcast_compare_fusion.3
  409.1 1.3 constant_dynamic-slice_fusion.4
  410.8 2.7 fusion.136
  413.5 3.0 fusion.137
  416.6 5.1 fusion.139
  421.7 1.6 copy-done.4
  423.4 2.4 divide_bitcast_fusion
  425.8 1.2 copy.34
  427.0 2.4 reshape.141
  429.4 20.1 %fusion.93 = (f32[4,4,512]{2,1,0:T(4,128)S(1)}, bf16[4,4,512,1024]{2,3,1,0:T(8,128)(2,1)}) fusion(bf16[1024,4,128,1]{0,2,3,1:T(8,128)(2,1)S(1)} %bitcast.156, pred[512,1024]{0,1:T(8,128)(4,1)S(1)} %copy-done.7, bf16[512,4,4,128]{3,2,1,0:T(4,128)(2,1)} %reshape.138), kind=kOutput, calls=%fused_computation.88 | convolution fusion | flops 2197816320 | bytes 20480000 | tf_op jit(solution)/shard_map/sub | solution.py:43
  449.5 9.5 %fusion.41 = bf16[512,4,4,128]{0,3,2,1:T(8,128)(2,1)} fusion(bf16[1024,4,128,1]{0,2,3,1:T(8,128)(2,1)S(1)} %bitcast.154, bf16[4,4,512,1024]{2,3,1,0:T(8,128)(2,1)} %get-tuple-element.136, f32[512,4,4]{0,2,1:T(4,128)S(1)} %bitcast.158), kind=kOutput, calls=%fused_computation.53 | convolution fusion | flops 2149580800 | bytes 19955712 | tf_op jit(solution)/shard_map/hgbk,khd->hgbd/dot_general | solution.py:22
  459.0 4.1 copy.31
  463.1 20.9 %fusion.98 = (f32[4,4,512]{2,1,0:T(4,128)S(1)}, bf16[4,4,512,1024]{2,3,1,0:T(8,128)(2,1)}) fusion(bf16[1024,4,128,1]{0,2,3,1:T(8,128)(2,1)} %bitcast.155, pred[512,1024]{0,1:T(8,128)(4,1)S(1)} %copy-done.6, bf16[512,4,4,128]{3,2,1,0:T(4,128)(2,1)S(1)} %copy-done.5), kind=kOutput, calls=%fused_computation.89 | convolution fusion | flops 2197816320 | bytes 20480000 | tf_op jit(solution)/shard_map/sub | solution.py:43
  484.0 8.5 %fusion.42 = bf16[512,4,4,128]{0,3,2,1:T(8,128)(2,1)S(1)} fusion(bf16[1024,4,128,1]{0,2,3,1:T(8,128)(2,1)} %bitcast.153, bf16[4,4,512,1024]{2,3,1,0:T(8,128)(2,1)} %get-tuple-element.138, f32[512,4,4]{0,2,1:T(4,128)S(1)} %bitcast.157), kind=kOutput, calls=%fused_computation.55 | convolution fusion | flops 2149580800 | bytes 19955712 | tf_op jit(solution)/shard_map/hgbk,khd->hgbd/dot_general | solution.py:22
  492.5 2.4 copy.30
  494.9 3.0 select_convert_fusion
  497.9 4.2 pad_maximum_fusion
  (114 shorter events, 13.9 us)
Async XLA Ops:
  7.2 68.2 %copy-start = (bf16[1,384,4096]{2,1,0:T(8,128)(2,1)S(1)}, bf16[1,384,4096]{2,1,0:T(8,128)(2,1)}, u32[]{:S(2)}) copy-start(bf16[1,384,4096]{2,1,0:T(8,128)(2,1)} %param.11) | copy-start | bytes 9437188
  7.2 68.2 %all-gather.10.cloned.1.call-start = ((), (), s32[]{:S(2)}) async-start(), calls=%async_computation.2 | async-start | bytes 4325376 | tf_op jit(solution)/shard_map/all_gather | solution.py:63
  7.9 130.9 %all-gather.6.cloned.1.call-start = ((), (), s32[]{:S(2)}) async-start(), calls=%async_computation | async-start | bytes 4325376 | tf_op jit(solution)/shard_map/all_gather | solution.py:62
  8.7 246.3 %all-gather.8.cloned.1.call-start = ((), (), s32[]{:S(2)}) async-start(), calls=%async_computation.1 | async-start | bytes 17301504 | tf_op jit(solution)/shard_map/all_gather | solution.py:61
  9.4 72.0 %copy-start.8 = (s32[1,1024]{1,0:T(1,128)S(1)}, s32[1,1024]{1,0:T(1,128)}, u32[]{:S(2)}) copy-start(s32[1,1024]{1,0:T(1,128)} %param.10) | copy-start | bytes 12292
  9.4 294.0 %all-gather.14.cloned.1.call-start = ((), (), s32[]{:S(2)}) async-start(), calls=%async_computation.4 | async-start | bytes 3538944 | tf_op jit(solution)/shard_map/all_gather | solution.py:89
  80.1 241.0 %all-gather.12.cloned.1.call-start = ((), (), s32[]{:S(2)}) async-start(), calls=%async_computation.3 | async-start | bytes 3538944 | tf_op jit(solution)/shard_map/all_gather | solution.py:88
  143.6 10.3 %copy-start.10 = (bf16[4096,512]{1,0:T(8,128)(2,1)S(1)}, bf16[4096,512]{1,0:T(8,128)(2,1)}, u32[]{:S(2)}) copy-start(bf16[4096,512]{1,0:T(8,128)(2,1)} %all-gather.6.cloned.1.call-done) | copy-start | bytes 12582916
  328.5 3.1 copy-start.3
  336.7 1.7 copy-start.4
  345.5 3.1 copy-start.3
  353.7 1.7 copy-start.4
  362.5 3.1 copy-start.3
  370.7 1.7 copy-start.4
  379.5 3.1 copy-start.3
  387.7 1.7 copy-start.4
  396.5 3.1 copy-start.3
  404.7 1.7 copy-start.4
  413.5 3.1 copy-start.3
  421.7 1.7 copy-start.4
  425.8 3.6 copy-start.7
  425.8 3.6 copy-start.12
  429.4 20.1 %copy-start.11 = (bf16[1024,512]{0,1:T(8,128)(2,1)S(1)}, bf16[1024,512]{0,1:T(8,128)(2,1)}, u32[]{:S(2)}) copy-start(bf16[1024,512]{0,1:T(8,128)(2,1)} %fusion.78) | copy-start | bytes 3145732
  459.0 4.1 copy-start.5
  459.0 4.1 copy-start.6
  492.5 2.4 copy-start.9
  494.9 3.0 copy-start.2
  494.9 7.2 %copy-start.1 = (bf16[1,384,4096]{2,1,0:T(8,128)(2,1)S(1)}, bf16[1,384,4096]{2,1,0:T(8,128)(2,1)}, u32[]{:S(2)}) copy-start(bf16[1,384,4096]{2,1,0:T(8,128)(2,1)} %param.11) | copy-start | bytes 9437188
Sparse Core Ops, SparseCore 0:
  11.0 64.3 all-gather.9
  78.4 60.4 all-gather.5
  141.8 113.1 all-gather.7
  256.7 30.3 all-gather.13
  288.9 32.1 all-gather.11
where the time goes:
time: 515 us; the launch traced here: 509 us
  waiting for transfers between devices  234 us (45%)
  matrix products  168 us (33%)
  local copies, waits for them, and re-layouts  48 us (9%)
  other arithmetic  43.3 us (8%)
  between operations  14.8 us (3%)
    all_gather x1, waiting for transfers between devices, local(): lax.all_gather(w_query, ('blk', 'dp'), axis=0, tiled=True)  92.7 us
    all_gather x1, waiting for transfers between devices, local(): lax.all_gather(w_value, ('blk', 'dp'), axis=0, tiled=True)  65.9 us
    all_gather x1, waiting for transfers between devices, local(): lax.all_gather(w_key, ('blk', 'dp'), axis=0, tiled=True)  55.5 us
    dot_general x8, matrix products, weighted_values(): jnp.einsum('hgbk,khd->hgbd', probabilities, value_heads, preferred_elemen...  48.3 us
    dot_general x3, matrix products, local(): jnp.dot(whole_rows, pieces[i], preferred_element_type=jnp.float32)  41.3 us
    sub x2, matrix products, short_attention(): exponentials = jnp.where(visible, jnp.exp(scores - row_max), 0.0)  41 us
    dot_general x3, matrix products, local(): jnp.dot(long_rows, pieces[i], preferred_element_type=jnp.float32)  21.1 us
    reduce_sum x6, other arithmetic, update(): running_sum = running_sum * rescale + jnp.sum(exponentials, axis=-1)  18.2 us
  transfers between devices with their start and end apart: 5, of which 4 were waited for; matrix products, arithmetic and copies ran while one was open for 16% of the time, Pallas kernels for 0%

commit v1 on v0

--- a/solution.py
+++ b/solution.py
@@ -6,6 +6,18 @@
 
 HD = 128
 masked_score = -1e30
+
+
+def collect(x, axis, dim):
+    ways, here, step = (lax.axis_size(axis), lax.axis_index(axis), x.shape[dim])
+    line, have = (x, 1)
+    while have < ways:
+        line = jnp.concatenate(
+            [line, lax.ppermute(line, axis, [(d, (d - have) % ways) for d in range(ways)])],
+            axis=dim,
+        )
+        have = 2 * have
+    return jnp.roll(line, here * step, axis=dim)
 
 
 def head_scores(query_rows, key_rows, kv_heads):
@@ -58,7 +70,7 @@
     kv_cols = w_key.shape[1]
     whole_rows = lax.all_gather(short_rows, "uly", axis=0, tiled=True)
     pieces = (
-        lax.all_gather(w_query, ("blk", "dp"), axis=0, tiled=True),
+        collect(w_query, ("blk", "dp"), 0),
         lax.all_gather(w_key, ("blk", "dp"), axis=0, tiled=True),
         lax.all_gather(w_value, ("blk", "dp"), axis=0, tiled=True),
     )

time: 515 us -> 773 us (1.50)
  waiting for transfers between devices: 234 us -> 366 us
  matrix products: 168 us -> 215 us
  local copies, waits for them, and re-layouts: 48 us -> 83.9 us
  other arithmetic: 43.3 us -> 72.1 us
  starting transfers between devices: 0.19 us -> 12.4 us
    ppermute x0 -> x5, waiting for transfers between devices: none -> 320 us  [collect(): lax.ppermute(line, axis, [(d, (d - have) % ways) for d in range(ways)])]
    all_gather x1 -> x0, waiting for transfers between devices: 92.7 us -> none  [local(): lax.all_gather(w_query, ('blk', 'dp'), axis=0, tiled=True)]
    all_gather x1, waiting for transfers between devices: 55.5 us -> 0.01 us  [local(): lax.all_gather(w_key, ('blk', 'dp'), axis=0, tiled=True)]
    unnamed x22 -> x37, local copies, waits for them, and re-layouts: 0.05 us -> 28.6 us
    dot_general x8, matrix products: 48.3 us -> 71.6 us  [weighted_values(): jnp.einsum('hgbk,khd->hgbd', probabilities, value_heads, preferred_elemen...]
    all_gather x1, waiting for transfers between devices: 65.9 us -> 45.1 us  [local(): lax.all_gather(w_value, ('blk', 'dp'), axis=0, tiled=True)]
    reduce_sum x6, other arithmetic: 18.2 us -> 38.8 us  [update(): running_sum = running_sum * rescale + jnp.sum(exponentials, axis=-1)]
    dot_general x6, matrix products: 16.1 us -> 36 us  [head_scores(): jnp.einsum('bhgd,khd->hgbk', query_heads, key_heads, preferred_element_ty...]
  transfers between devices with their start and end apart: 5 -> 9, of which waited for: 4 -> 6; matrix products, arithmetic and copies ran while one was open for 16% -> 16% of each run, Pallas kernels for 0% -> 0%
where the time goes in v1:
time: 773 us; the launch traced here: 764 us
  waiting for transfers between devices  366 us (47%)
  matrix products  215 us (28%)
  local copies, waits for them, and re-layouts  83.9 us (11%)
  other arithmetic  72.1 us (9%)
  between operations  14.9 us (2%)
  starting transfers between devices  12.4 us (2%)
    ppermute x5, waiting for transfers between devices, collect(): lax.ppermute(line, axis, [(d, (d - have) % ways) for d in range(ways)])  320 us
    dot_general x8, matrix products, weighted_values(): jnp.einsum('hgbk,khd->hgbd', probabilities, value_heads, preferred_elemen...  71.6 us
    all_gather x1, waiting for transfers between devices, local(): lax.all_gather(w_value, ('blk', 'dp'), axis=0, tiled=True)  45.1 us
    dot_general x3, matrix products, local(): jnp.dot(whole_rows, pieces[i], preferred_element_type=jnp.float32)  43.2 us
    sub x2, matrix products, short_attention(): exponentials = jnp.where(visible, jnp.exp(scores - row_max), 0.0)  41.2 us
    reduce_sum x6, other arithmetic, update(): running_sum = running_sum * rescale + jnp.sum(exponentials, axis=-1)  38.8 us
    dot_general x6, matrix products, head_scores(): jnp.einsum('bhgd,khd->hgbk', query_heads, key_heads, preferred_element_ty...  36 us
    unnamed x37, local copies, waits for them, and re-layouts  28.6 us
  transfers between devices with their start and end apart: 9, of which 6 were waited for; matrix products, arithmetic and copies ran while one was open for 16% of the time, Pallas kernels for 0%

profile of v1, /device:TPU:0, one launch (start us, length us, event | category | flops | bytes accessed | tf_op | source)
XLA Modules:
  0.0 764.5 jit_solution(9561387752789478007)
XLA Ops:
  8.0 6.5 collective-permute-start
  14.5 11.6 %collective-permute-done = bf16[128,2048]{1,0:T(8,128)(2,1)} collective-permute-done((bf16[128,2048]{1,0:T(8,128)(2,1)}, bf16[128,2048]{1,0:T(8,128)(2,1)}, u32[]{:S(2)}, u32[]{:S(2)}) %collective-permute-start) | collective-permute-done | bytes 524320 | tf_op jit(solution)/shard_map/ppermute | solution.py:16
  27.9 52.9 %collective-permute-done.1 = bf16[256,2048]{1,0:T(8,128)(2,1)S(1)} collective-permute-done((bf16[256,2048]{1,0:T(8,128)(2,1)S(1)}, bf16[256,2048]{1,0:T(8,128)(2,1)S(1)}, u32[]{:S(2)}, u32[]{:S(2)}) %collective-permute-start.1) | collective-permute-done | bytes 1048608 | tf_op jit(solution)/shard_map/ppermute | solution.py:16
  80.8 1.8 pad_maximum_fusion.2
  82.6 3.4 collective-permute-start.2
  85.9 31.1 %collective-permute-done.2 = bf16[512,2048]{1,0:T(8,128)(2,1)S(1)} collective-permute-done((bf16[512,2048]{1,0:T(8,128)(2,1)S(1)}, bf16[512,2048]{1,0:T(8,128)(2,1)S(1)}, u32[]{:S(2)}, u32[]{:S(2)}) %collective-permute-start.2) | collective-permute-done | bytes 2097184 | tf_op jit(solution)/shard_map/ppermute | solution.py:16
  117.0 3.6 pad_maximum_fusion
  122.8 2.2 constant_dynamic-update-slice_fusion.3
  124.9 1.6 constant_dynamic-update-slice_fusion.2
  126.6 2.5 constant_dynamic-update-slice_fusion.1
  129.1 4.7 fusion.77
  133.9 80.5 %collective-permute-done.3 = bf16[1024,2048]{1,0:T(8,128)(2,1)} collective-permute-done((bf16[1024,2048]{1,0:T(8,128)(2,1)}, bf16[1024,2048]{1,0:T(8,128)(2,1)}, u32[]{:S(2)}, u32[]{:S(2)}) %collective-permute-start.3) | collective-permute-done | bytes 4194336 | tf_op jit(solution)/shard_map/ppermute | solution.py:16
  214.3 6.8 constant_dynamic-update-slice_fusion
  223.3 1.9 fusion.69
  225.2 45.1 %all-gather.7.cloned.1.call-done = bf16[4096,512]{1,0:T(8,128)(2,1)} async-done(((bf16[128,512]{1,0:T(8,128)(2,1)}), bf16[4096,512]{1,0:T(8,128)(2,1)}) %all-gather.7.cloned.1.call-update) | async-done | bytes 4194320 | tf_op jit(solution)/shard_map/all_gather | solution.py:75
  270.4 4.7 fusion.80
  275.1 10.7 %fusion.71 = bf16[1024,512]{0,1:T(8,128)(2,1)} fusion(bf16[4096,512]{1,0:T(8,128)(2,1)} %all-gather.5.cloned.1.call-done, bf16[1,1024,4096]{2,1,0:T(8,128)(2,1)} %param.9), kind=kOutput, calls=%fused_computation.75 | convolution fusion | flops 4295491584 | bytes 13631488 | tf_op jit(solution)/shard_map/dot_general | solution.py:78
  285.8 8.4 %fusion.74 = bf16[1024,512]{0,1:T(8,128)(2,1)} fusion(bf16[4096,512]{1,0:T(8,128)(2,1)S(1)} %copy-done.12, bf16[1,1024,4096]{2,1,0:T(8,128)(2,1)} %param.9), kind=kOutput, calls=%fused_computation.76 | convolution fusion | flops 4295491584 | bytes 13631488 | tf_op jit(solution)/shard_map/dot_general | solution.py:78
  294.3 144.1 %collective-permute-done.4 = bf16[2048,2048]{1,0:T(8,128)(2,1)} collective-permute-done((bf16[2048,2048]{1,0:T(8,128)(2,1)}, bf16[2048,2048]{1,0:T(8,128)(2,1)}, u32[]{:S(2)}, u32[]{:S(2)}) %collective-permute-start.4) | collective-permute-done | bytes 8388640 | tf_op jit(solution)/shard_map/ppermute | solution.py:16
  438.3 8.4 %constant_dynamic-update-slice_fusion.11 = bf16[8192,2048]{1,0:T(8,128)(2,1)} fusion(bf16[8192,2048]{1,0:T(8,128)(2,1)} %get-tuple-element.142, bf16[2048,2048]{1,0:T(8,128)(2,1)} %collective-permute-done.4), kind=kLoop, calls=%fused_computation.91 | loop fusion | bytes 16777216
  446.8 1.9 constant_dynamic-update-slice_fusion.10
  448.6 1.9 constant_dynamic-update-slice_fusion.9
  451.6 1.4 constant_dynamic-update-slice_fusion.7
  453.0 4.8 constant_dynamic-update-slice_fusion.6
  457.8 8.3 %constant_dynamic-update-slice_fusion.5 = bf16[8192,2048]{1,0:T(8,128)(2,1)} fusion(bf16[8192,2048]{1,0:T(8,128)(2,1)} %constant_dynamic-update-slice_fusion.6, bf16[2048,2048]{1,0:T(8,128)(2,1)} %collective-permute-done.4), kind=kLoop, calls=%fused_computation.85 | loop fusion | bytes 16777216 | tf_op jit(solution)/shard_map/jit(_roll_dynamic)/concatenate | solution.py:20
  466.1 13.3 %fusion.60 = bf16[384,2048]{0,1:T(8,128)(2,1)} fusion(bf16[1,384,4096]{2,1,0:T(8,128)(2,1)S(1)} %copy-done, bf16[8192,2048]{1,0:T(8,128)(2,1)} %constant_dynamic-update-slice_fusion.5, s32[]{:T(128)S(6)} %select_n.45), kind=kOutput, calls=%fused_computation.69 | convolution fusion | flops 6443237376 | bytes 21495812 | tf_op jit(solution)/shard_map/dot_general | solution.py:81
  479.4 1.7 copy.34
  482.3 24.1 %convert_bitcast_fusion = bf16[1024,2048]{0,1:T(8,128)(2,1)} fusion(bf16[1,1024,4096]{2,1,0:T(8,128)(2,1)} %param.9, bf16[8192,2048]{1,0:T(8,128)(2,1)} %constant_dynamic-update-slice_fusion.5, s32[]{:T(128)S(6)} %select_n.45), kind=kOutput, calls=%fused_computation.60 | convolution fusion | flops 17181966336 | bytes 29360132 | tf_op jit(solution)/shard_map/dot_general | solution.py:78
  506.4 167.2 %while.16 = (s32[]{:T(128)}, f32[4,4,384]{2,1,0:T(4,128)S(1)}, f32[4,4,384]{2,1,0:T(4,128)S(1)}, f32[4,4,384,128]{3,2,1,0:T(8,128)}, s32[6]{0:T(128)S(1)}, /*ind...) while((s32[]{:T(128)}, f32[4,4,384]{2,1,0:T(4,128)S(1)}, ...), condition=%wide.wide.region_7.8_spmd.clone, body=%wide.wide.region_4.7_spmd.clone.sunk | while | flops 1654292352 | bytes 52043940 | solution.py:128
  509.4 2.1 constant_dynamic-slice_fusion.4
  512.7 6.0 fusion.128
  518.7 6.5 fusion.129
  525.4 8.5 %fusion.131 = f32[4,4,384,128]{3,2,1,0:T(8,128)} fusion(f32[4,4,384,128]{3,2,1,0:T(8,128)} %get-tuple-element.304, bf16[512,4,128,1]{0,2,3,1:T(8,128)(2,1)S(1)} %bitcast.155, f32[4,512,384,4]{2,1,3,0:T(8,128)} %get-tuple-element.284, f32[4,4,384]{2,1,0:T(4,128)S(1)} %select_maximum_fusion.3, pred[384,512]{0,1:T(8,128)(4,1)S(1)} %compare_and_fusion.3, ...), kind=kOutput, calls=%fused_computation.9.clone.clone.1 | convolution fusion | flops 823394304 | bytes 19644416 | tf_op jit(solution)/shard_map/while/body/eval_jaxpr/hgbk,khd->hgbd/dot_general | solution.py:34
  536.8 2.1 constant_dynamic-slice_fusion.4
  540.2 6.0 fusion.128
  546.2 6.5 fusion.129
  552.9 8.9 %fusion.131 = f32[4,4,384,128]{3,2,1,0:T(8,128)} fusion(f32[4,4,384,128]{3,2,1,0:T(8,128)} %get-tuple-element.304, bf16[512,4,128,1]{0,2,3,1:T(8,128)(2,1)S(1)} %bitcast.155, f32[4,512,384,4]{2,1,3,0:T(8,128)} %get-tuple-element.284, f32[4,4,384]{2,1,0:T(4,128)S(1)} %select_maximum_fusion.3, pred[384,512]{0,1:T(8,128)(4,1)S(1)} %compare_and_fusion.3, ...), kind=kOutput, calls=%fused_computation.9.clone.clone.1 | convolution fusion | flops 823394304 | bytes 19644416 | tf_op jit(solution)/shard_map/while/body/eval_jaxpr/hgbk,khd->hgbd/dot_general | solution.py:34
  564.8 2.1 constant_dynamic-slice_fusion.4
  568.1 6.0 fusion.128
  574.1 6.5 fusion.129
  580.9 8.9 %fusion.131 = f32[4,4,384,128]{3,2,1,0:T(8,128)} fusion(f32[4,4,384,128]{3,2,1,0:T(8,128)} %get-tuple-element.304, bf16[512,4,128,1]{0,2,3,1:T(8,128)(2,1)S(1)} %bitcast.155, f32[4,512,384,4]{2,1,3,0:T(8,128)} %get-tuple-element.284, f32[4,4,384]{2,1,0:T(4,128)S(1)} %select_maximum_fusion.3, pred[384,512]{0,1:T(8,128)(4,1)S(1)} %compare_and_fusion.3, ...), kind=kOutput, calls=%fused_computation.9.clone.clone.1 | convolution fusion | flops 823394304 | bytes 19644416 | tf_op jit(solution)/shard_map/while/body/eval_jaxpr/hgbk,khd->hgbd/dot_general | solution.py:34
  592.7 2.1 constant_dynamic-slice_fusion.4
  596.1 6.0 fusion.128
  602.1 6.5 fusion.129
  608.8 8.9 %fusion.131 = f32[4,4,384,128]{3,2,1,0:T(8,128)} fusion(f32[4,4,384,128]{3,2,1,0:T(8,128)} %get-tuple-element.304, bf16[512,4,128,1]{0,2,3,1:T(8,128)(2,1)S(1)} %bitcast.155, f32[4,512,384,4]{2,1,3,0:T(8,128)} %get-tuple-element.284, f32[4,4,384]{2,1,0:T(4,128)S(1)} %select_maximum_fusion.3, pred[384,512]{0,1:T(8,128)(4,1)S(1)} %compare_and_fusion.3, ...), kind=kOutput, calls=%fused_computation.9.clone.clone.1 | convolution fusion | flops 823394304 | bytes 19644416 | tf_op jit(solution)/shard_map/while/body/eval_jaxpr/hgbk,khd->hgbd/dot_general | solution.py:34
  620.6 2.1 constant_dynamic-slice_fusion.4
  624.0 6.0 fusion.128
  630.0 6.5 fusion.129
  636.7 8.9 %fusion.131 = f32[4,4,384,128]{3,2,1,0:T(8,128)} fusion(f32[4,4,384,128]{3,2,1,0:T(8,128)} %get-tuple-element.304, bf16[512,4,128,1]{0,2,3,1:T(8,128)(2,1)S(1)} %bitcast.155, f32[4,512,384,4]{2,1,3,0:T(8,128)} %get-tuple-element.284, f32[4,4,384]{2,1,0:T(4,128)S(1)} %select_maximum_fusion.3, pred[384,512]{0,1:T(8,128)(4,1)S(1)} %compare_and_fusion.3, ...), kind=kOutput, calls=%fused_computation.9.clone.clone.1 | convolution fusion | flops 823394304 | bytes 19644416 | tf_op jit(solution)/shard_map/while/body/eval_jaxpr/hgbk,khd->hgbd/dot_general | solution.py:34
  648.6 2.1 constant_dynamic-slice_fusion.4
  651.9 6.0 fusion.128
  657.9 6.5 fusion.129
  664.7 8.9 %fusion.131 = f32[4,4,384,128]{3,2,1,0:T(8,128)} fusion(f32[4,4,384,128]{3,2,1,0:T(8,128)} %get-tuple-element.304, bf16[512,4,128,1]{0,2,3,1:T(8,128)(2,1)S(1)} %bitcast.155, f32[4,512,384,4]{2,1,3,0:T(8,128)} %get-tuple-element.284, f32[4,4,384]{2,1,0:T(4,128)S(1)} %select_maximum_fusion.3, pred[384,512]{0,1:T(8,128)(4,1)S(1)} %compare_and_fusion.3, ...), kind=kOutput, calls=%fused_computation.9.clone.clone.1 | convolution fusion | flops 823394304 | bytes 19644416 | tf_op jit(solution)/shard_map/while/body/eval_jaxpr/hgbk,khd->hgbd/dot_general | solution.py:34
  673.6 2.8 divide_bitcast_fusion
  677.6 2.4 reshape.141
  680.0 3.8 fusion.89
  683.8 20.4 %fusion.92 = (f32[4,4,512]{2,1,0:T(4,128)S(1)}, bf16[4,4,512,1024]{2,3,1,0:T(8,128)(2,1)}) fusion(bf16[1024,4,128,1]{0,2,3,1:T(8,128)(2,1)} %bitcast.167, bf16[512,4,4,128]{0,3,2,1:T(8,128)(2,1)S(1)} %bitcast.161, pred[512,1024]{0,1:T(8,128)(4,1)S(1)} %copy-done.9), kind=kOutput, calls=%fused_computation.108 | convolution fusion | flops 2197816320 | bytes 20480000 | tf_op jit(solution)/shard_map/sub | solution.py:55
  704.3 8.5 %fusion.45 = bf16[512,4,4,128]{0,3,2,1:T(8,128)(2,1)S(1)} fusion(bf16[1024,4,128,1]{0,2,3,1:T(8,128)(2,1)} %bitcast.165, bf16[4,4,512,1024]{2,3,1,0:T(8,128)(2,1)} %get-tuple-element.158, f32[512,4,4]{0,2,1:T(4,128)S(1)} %bitcast.170), kind=kOutput, calls=%fused_computation.59 | convolution fusion | flops 2149580800 | bytes 19955712 | tf_op jit(solution)/shard_map/hgbk,khd->hgbd/dot_general | solution.py:34
  712.8 2.5 copy.31
  715.3 20.8 %fusion.91 = (f32[4,4,512]{2,1,0:T(4,128)S(1)}, bf16[4,4,512,1024]{2,3,1,0:T(8,128)(2,1)}) fusion(bf16[1024,4,128,1]{0,2,3,1:T(8,128)(2,1)} %bitcast.168, bf16[512,4,4,128]{0,3,2,1:T(8,128)(2,1)} %bitcast.160, pred[512,1024]{0,1:T(8,128)(4,1)S(1)} %copy-done.8), kind=kOutput, calls=%fused_computation.107 | convolution fusion | flops 2197816320 | bytes 20480000 | tf_op jit(solution)/shard_map/sub | solution.py:55
  736.1 9.9 %fusion.44 = bf16[512,4,4,128]{0,3,2,1:T(8,128)(2,1)} fusion(bf16[1024,4,128,1]{0,2,3,1:T(8,128)(2,1)} %bitcast.166, bf16[4,4,512,1024]{2,3,1,0:T(8,128)(2,1)} %get-tuple-element.156, f32[512,4,4]{0,2,1:T(4,128)S(1)} %bitcast.169), kind=kOutput, calls=%fused_computation.57 | convolution fusion | flops 2149580800 | bytes 19955712 | tf_op jit(solution)/shard_map/hgbk,khd->hgbd/dot_general | solution.py:34
  746.1 4.0 copy.32
  750.0 2.9 select_convert_fusion
  752.9 4.8 pad_maximum_fusion.1
  (115 shorter events, 36.0 us)
Async XLA Ops:
  7.2 121.9 %copy-start = (bf16[1,384,4096]{2,1,0:T(8,128)(2,1)S(1)}, bf16[1,384,4096]{2,1,0:T(8,128)(2,1)}, u32[]{:S(2)}) copy-start(bf16[1,384,4096]{2,1,0:T(8,128)(2,1)} %param.11) | copy-start | bytes 9437188
  7.2 121.9 %all-gather.5.cloned.1.call-start = ((), (), s32[]{:S(2)}) async-start(), calls=%async_computation | async-start | bytes 4325376 | tf_op jit(solution)/shard_map/all_gather | solution.py:74
  7.9 262.5 %all-gather.7.cloned.1.call-start = ((), (), s32[]{:S(2)}) async-start(), calls=%async_computation.1 | async-start | bytes 4325376 | tf_op jit(solution)/shard_map/all_gather | solution.py:75
  8.0 18.2 %collective-permute-start = (bf16[128,2048]{1,0:T(8,128)(2,1)}, bf16[128,2048]{1,0:T(8,128)(2,1)}, u32[]{:S(2)}, u32[]{:S(2)}) collective-permute-start(bf16[128,2048]{1,0:T(8,128)(2,1)} %param.13), channel_id=1, source_target_pairs={{0,31},{1,0},{2,1},{3,2},{4,3},{5,4},{6,5},{7,6},{8,7},{9,8},{10,9... | collective-permute-start | bytes 1572872 | tf_op jit(solution)/shard_map/ppermute | solution.py:16
  14.4 492.0 %all-gather.9.cloned.1.call-start = ((), (), s32[]{:S(2)}) async-start(), calls=%async_computation.2 | async-start | bytes 3538944 | tf_op jit(solution)/shard_map/all_gather | solution.py:100
  14.5 107.2 %copy-start.6 = (bf16[128,2048]{1,0:T(8,128)(2,1)S(1)}, bf16[128,2048]{1,0:T(8,128)(2,1)}, u32[]{:S(2)}) copy-start(bf16[128,2048]{1,0:T(8,128)(2,1)} %param.13) | copy-start | bytes 1572868
  27.4 53.4 %collective-permute-start.1 = (bf16[256,2048]{1,0:T(8,128)(2,1)S(1)}, bf16[256,2048]{1,0:T(8,128)(2,1)S(1)}, u32[]{:S(2)}, u32[]{:S(2)}) collective-permute-start(bf16[256,2048]{1,0:T(8,128)(2,1)S(1)} %pad_maximum_fusion.3), channel_id=1, source_target_pairs={{0,30},{1,31},{2,0},{3,1},{4,2},{5,3},{6,4},{7,5},{8,6},{9,7},{10,... | collective-permute-start | bytes 3145736 | tf_op jit(solution)/shard_map/ppermute | solution.py:16
  80.8 45.8 %copy-start.4 = (bf16[256,2048]{1,0:T(8,128)(2,1)}, bf16[256,2048]{1,0:T(8,128)(2,1)S(1)}, u32[]{:S(2)}) copy-start(bf16[256,2048]{1,0:T(8,128)(2,1)S(1)} %collective-permute-done.1) | copy-start | bytes 3145732
  82.6 34.5 %collective-permute-start.2 = (bf16[512,2048]{1,0:T(8,128)(2,1)S(1)}, bf16[512,2048]{1,0:T(8,128)(2,1)S(1)}, u32[]{:S(2)}, u32[]{:S(2)}) collective-permute-start(bf16[512,2048]{1,0:T(8,128)(2,1)S(1)} %pad_maximum_fusion.2), channel_id=1, source_target_pairs={{0,28},{1,29},{2,30},{3,31},{4,0},{5,1},{6,2},{7,3},{8,4},{9,5},{1... | collective-permute-start | bytes 6291464 | tf_op jit(solution)/shard_map/ppermute | solution.py:16
  117.0 9.5 %copy-start.2 = (bf16[512,2048]{1,0:T(8,128)(2,1)}, bf16[512,2048]{1,0:T(8,128)(2,1)S(1)}, u32[]{:S(2)}) copy-start(bf16[512,2048]{1,0:T(8,128)(2,1)S(1)} %collective-permute-done.2) | copy-start | bytes 6291460
  120.7 93.6 %collective-permute-start.3 = (bf16[1024,2048]{1,0:T(8,128)(2,1)}, bf16[1024,2048]{1,0:T(8,128)(2,1)}, u32[]{:S(2)}, u32[]{:S(2)}) collective-permute-start(bf16[1024,2048]{1,0:T(8,128)(2,1)} %pad_maximum_fusion), channel_id=1, source_target_pairs={{0,24},{1,25},{2,26},{3,27},{4,28},{5,29},{6,30},{7,31},{8,0},{9,1... | collective-permute-start | bytes 12582920 | tf_op jit(solution)/shard_map/ppermute | solution.py:16
  133.8 89.5 %copy-start.10 = (s32[1,1024]{1,0:T(1,128)S(1)}, s32[1,1024]{1,0:T(1,128)}, u32[]{:S(2)}) copy-start(s32[1,1024]{1,0:T(1,128)} %param.10) | copy-start | bytes 12292
  133.8 372.6 %all-gather.11.cloned.1.call-start = ((), (), s32[]{:S(2)}) async-start(), calls=%async_computation.3 | async-start | bytes 3538944 | tf_op jit(solution)/shard_map/all_gather | solution.py:101
  221.1 217.2 %collective-permute-start.4 = (bf16[2048,2048]{1,0:T(8,128)(2,1)}, bf16[2048,2048]{1,0:T(8,128)(2,1)}, u32[]{:S(2)}, u32[]{:S(2)}) collective-permute-start(bf16[2048,2048]{1,0:T(8,128)(2,1)} %get-tuple-element.141), channel_id=1, source_target_pairs={{0,16},{1,17},{2,18},{3,19},{4,20},{5,21},{6,22},{7,23},{8,24},{9,... | collective-permute-start | bytes 25165832 | tf_op jit(solution)/shard_map/ppermute | solution.py:16
  275.1 10.7 %copy-start.12 = (bf16[4096,512]{1,0:T(8,128)(2,1)S(1)}, bf16[4096,512]{1,0:T(8,128)(2,1)}, u32[]{:S(2)}) copy-start(bf16[4096,512]{1,0:T(8,128)(2,1)} %all-gather.7.cloned.1.call-done) | copy-start | bytes 12582916
  438.3 12.2 %copy-start.5 = (bf16[256,2048]{1,0:T(8,128)(2,1)S(1)}, bf16[256,2048]{1,0:T(8,128)(2,1)}, u32[]{:S(2)}) copy-start(bf16[256,2048]{1,0:T(8,128)(2,1)} %copy-done.4) | copy-start | bytes 3145732
  438.3 13.2 %copy-start.3 = (bf16[512,2048]{1,0:T(8,128)(2,1)S(1)}, bf16[512,2048]{1,0:T(8,128)(2,1)}, u32[]{:S(2)}) copy-start(bf16[512,2048]{1,0:T(8,128)(2,1)} %copy-done.2) | copy-start | bytes 6291460
  481.2 25.3 %copy-start.7 = (bf16[384,2048]{1,0:T(8,128)(2,1)}, bf16[384,2048]{1,0:T(8,128)(2,1)S(1)}, u32[]{:S(2)}) copy-start(bf16[384,2048]{1,0:T(8,128)(2,1)S(1)} %copy.34) | copy-start | bytes 4718596
  677.6 6.2 copy-start.9
  704.3 11.0 %copy-start.8 = (pred[512,1024]{0,1:T(8,128)(4,1)S(1)}, pred[512,1024]{0,1:T(8,128)(4,1)}, u32[]{:S(2)}) copy-start(pred[512,1024]{0,1:T(8,128)(4,1)} %get-tuple-element.152) | copy-start | bytes 1572868
  736.1 13.9 %copy-start.11 = (pred[384]{0:T(512)(128)(4,1)S(1)}, pred[384]{0:T(512)(128)(4,1)}, u32[]{:S(2)}) copy-start(pred[384]{0:T(512)(128)(4,1)} %add_compare_fusion) | copy-start | bytes 1156
  736.1 21.6 %copy-start.1 = (bf16[1,384,4096]{2,1,0:T(8,128)(2,1)S(1)}, bf16[1,384,4096]{2,1,0:T(8,128)(2,1)}, u32[]{:S(2)}) copy-start(bf16[1,384,4096]{2,1,0:T(8,128)(2,1)} %param.11) | copy-start | bytes 9437188
Sparse Core Ops, SparseCore 0:
  11.0 98.6 all-gather.4
  112.7 157.6 all-gather.6
  272.3 43.8 all-gather.8
  317.9 45.0 all-gather.10
